TPU v7x, 32 devices: a whole 2x2x4 slice. The times are simulated.
32 devices in a mesh: ga: 2 (over x), row: 8 (over z, y), col: 2 (over core).
Axes of the slice: x: 2, y: 2, z: 4, core: 2. Of those that a mesh axis runs over, the one named last changes fastest.
Arguments:
- pair: bfloat16 [256, 128, 128], P(('ga', 'row', 'col')), parts along dimension 0, may hold values from -480 to 480
- residue_mask: int32 [256], P('ga'), parts along dimension 0, may hold values from 0 to 1, as said below
- targets: int32 [256, 128], P(('ga', 'row', 'col')), parts along dimension 0, may hold values from 0 to 63
- ln_gain: float32 [2, 128], replicated, may hold values from 0.25 to 1.75
- ln_shift: float32 [2, 128], replicated, may hold values from -3 to 3
- w_in: bfloat16 [5, 128, 128], P(None, None, 'col'), may hold values from -0.5 to 0.5
- b_in: float32 [5, 128], replicated, may hold values from -3 to 3
- w_out: bfloat16 [128, 128], P('col'), may hold values from -0.5 to 0.5
- b_out: float32 [128], replicated, may hold values from -3 to 3
- head_weight: bfloat16 [128, 64], replicated, may hold values from -0.5 to 0.5
- head_bias: float32 [64], replicated, may hold values from -4 to 4
Outputs:
- update: bfloat16 [256, 128, 128], P(('ga', 'row', 'col')), parts along dimension 0
- pair_loss: float32 [256, 128], P(('ga', 'row', 'col')), parts along dimension 0
There are 2 independent parts, one for each index of `ga`. A program takes and returns all parts, laid end to end along the dimension named above; an argument that names none is the same for every part. Nothing has to cross between parts.
Inputs may be any that keep to these rules, and one draw needn't show every extreme that they name: `residue_mask`: each part's entries are 1 for residues 0 to some length - 1 and 0 after it; the length is at least 64 and at most 128.
All inputs are finite; a program needn't handle non-finite values.
Results may differ from a plain program's by a relative error of at most 0.0055.
Values may be sent and summed in bfloat16 or wider, within the bound.
A program may use at most 64 MiB of HBM per device.

v0:
```python
import jax
import jax.numpy as jnp
from jax import lax
from jax.sharding import PartitionSpec as P


def normalize(values, gain_vec, shift_vec, epsilon, reduce_axis):
    average = jnp.mean(values, axis=reduce_axis, keepdims=True)
    centred = values - average
    spread = jnp.mean(centred * centred, axis=reduce_axis, keepdims=True)
    return centred * lax.rsqrt(spread + epsilon) * gain_vec + shift_vec


def local(
    pair, residue_mask, targets, ln_gain, ln_shift, w_in, b_in, w_out, b_out, head_weight, head_bias
):
    row_count, length, pair_width = pair.shape
    groups = lax.axis_size(("row", "col"))
    chan_share = pair_width // groups
    res_mask = residue_mask.astype(jnp.float32)
    own_mask = lax.dynamic_slice_in_dim(
        res_mask, lax.axis_index(("row", "col")) * row_count, row_count
    )
    pair_mask = own_mask[:, None] * res_mask[None, :]
    normed = normalize(pair.astype(jnp.float32), ln_gain[0], ln_shift[0], 0.1, -1).astype(
        jnp.bfloat16
    )
    projected = jnp.einsum(
        "ikc,ncd->ndik",
        normed,
        lax.all_gather(w_in, "col", axis=2, tiled=True),
        preferred_element_type=jnp.float32,
    )
    projected = projected + b_in[:, :, None, None]
    left_side = pair_mask * jax.nn.sigmoid(projected[1]) * projected[0]
    right_side = pair_mask * jax.nn.sigmoid(projected[3]) * projected[2]
    stacked = jnp.stack([left_side, right_side, projected[4]])
    left_side = stacked[0].astype(jnp.bfloat16)
    right_side = stacked[1].astype(jnp.bfloat16)
    gate_pre = stacked[2]
    left_blocks = left_side.reshape(groups, chan_share, row_count, length)
    right_blocks = right_side.reshape(groups, chan_share, row_count, length)
    left_part = lax.all_to_all(left_blocks, ("row", "col"), split_axis=0, concat_axis=2, tiled=True)
    right_part = lax.all_to_all(
        right_blocks, ("row", "col"), split_axis=0, concat_axis=2, tiled=True
    )
    product = jnp.einsum(
        "xcik,xcjk->xcij", left_part, right_part, preferred_element_type=jnp.float32
    )
    returned = lax.all_to_all(
        product.astype(jnp.bfloat16), ("row", "col"), split_axis=2, concat_axis=0, tiled=True
    )
    outer_prod = returned.reshape(pair_width, row_count, length)
    normed_outer = normalize(
        outer_prod.astype(jnp.float32),
        ln_gain[1][:, None, None],
        ln_shift[1][:, None, None],
        1.0,
        0,
    ).astype(jnp.bfloat16)
    mixed = jnp.einsum(
        "cij,cd->dij",
        normed_outer,
        lax.all_gather(w_out, "col", axis=0, tiled=True),
        preferred_element_type=jnp.float32,
    )
    update_chan = jax.nn.sigmoid(gate_pre) * (mixed + b_out[:, None, None])
    update = jnp.transpose(update_chan, (1, 2, 0)).astype(jnp.bfloat16)
    new_pair = (pair.astype(jnp.float32) + update.astype(jnp.float32)).astype(jnp.bfloat16)
    logits = (
        jnp.einsum("ijc,cb->ijb", new_pair, head_weight, preferred_element_type=jnp.float32)
        + head_bias
    )
    mirrored = lax.all_to_all(
        logits.astype(jnp.bfloat16), ("row", "col"), split_axis=1, concat_axis=0, tiled=True
    ).astype(logits.dtype)
    symmetric = logits + jnp.transpose(mirrored, (1, 0, 2))
    row_top = jnp.max(symmetric, axis=-1, keepdims=True)
    log_total = row_top[..., 0] + jnp.log(jnp.sum(jnp.exp(symmetric - row_top), axis=-1))
    bin_index = jnp.arange(symmetric.shape[2], dtype=jnp.int32)
    picked = jnp.sum(jnp.where(targets[..., None] == bin_index, symmetric, 0.0), axis=-1)
    pair_loss = pair_mask * (log_total - picked)
    return (update, pair_loss)


def solution(mesh):
    placed = (
        P(("ga", "row", "col"), None, None),
        P("ga"),
        P(("ga", "row", "col"), None),
        P(),
        P(),
        P(None, None, "col"),
        P(),
        P("col", None),
        P(),
        P(),
        P(),
    )
    return jax.shard_map(
        local,
        mesh=mesh,
        in_specs=placed,
        out_specs=(P(("ga", "row", "col"), None, None), P(("ga", "row", "col"), None)),
        check_vma=False,
    )
```

profile of v0, /device:TPU:0, one launch (start us, length us, event | category | flops | bytes accessed | tf_op | source)
XLA Modules:
  0.0 68.8 jit_solution(7911302540243961104)
XLA Ops:
  0.6 0.0 copy-start
  0.6 1.1 %copy.51 = bf16[8,128,128]{1,2,0:T(8,128)(2,1)S(1)} copy(bf16[8,128,128]{2,1,0:T(8,128)(2,1)} %param.11) | data formatting | bytes 524288 | tf_op args[0]
  1.8 0.1 fusion.7
  1.9 2.3 %all_gather.6 = bf16[5,128,128]{1,2,0:T(8,128)(2,1)S(1)} all-gather(bf16[5,128,64]{1,2,0:T(8,128)(2,1)} %param.16), channel_id=1, replica_groups=mesh['ga'=2,'row'=8,'col'=2] {'col'}, dimensions={2}, use_global_device_ids=true | all-gather | bytes 245760 | tf_op jit(solution)/shard_map/all_gather | solution.py:31
  4.2 0.8 %slice_bitcast_fusion.2 = (f32[128]{0:T(128)S(1)}, f32[128]{0:T(128)S(1)}, f32[128]{0:T(128)S(1)}, f32[128]{0:T(128)S(1)}) fusion(f32[2,128]{1,0:T(2,128)} %param.15, f32[2,128]{1,0:T(2,128)} %param.14), kind=kLoop, calls=%fused_computation.74 | loop fusion | bytes 4096 | tf_op jit(solution)/shard_map/add | solution.py:11
  5.0 1.3 %add_bitcast_fusion = f32[5,128,8,128]{3,1,0,2:T(8,128)S(1)} fusion(f32[5,128]{1,0:T(8,128)} %param.17, bf16[8,128,128]{1,2,0:T(8,128)(2,1)S(1)} %copy.51, f32[128]{0:T(128)S(1)} %get-tuple-element.21, f32[128]{0:T(128)S(1)} %get-tuple-element.24, f32[8,128]{1,0:T(8,128)S(1)} %add_rsqrt_fusion.1, f32[8,128]{1,0:T(8,128)S(1)} %broadcast_multiply_fusion.2, ...), kind=kOutput, calls=%fused_computation | convolution fusion | flops 169213952 | bytes 3059200 | tf_op jit(solution)/shard_map/ikc,ncd->ndik/dot_general | solution.py:28
  6.2 0.0 copy-start.4
  6.3 1.3 %fusion.19 = (f32[16,8,8,128]{3,1,0,2:T(8,128)S(1)}, f32[16,8,8,128]{3,1,0,2:T(8,128)}, f32[16,8,8,128]{3,1,0,2:T(8,128)}, f32[16,8,8,128]{3,1,0,2:T(8,128)}) fusion(f32[5,128,8,128]{3,1,0,2:T(8,128)S(1)} %add_bitcast_fusion), kind=kLoop, calls=%fused_computation.30 | loop fusion | flops 786432 | bytes 4194304 | tf_op jit(solution)/shard_map/div | solution.py:35
  7.6 0.0 copy-done.4
  7.6 0.1 dynamic_slice.3
  7.6 0.1 broadcast_multiply_fusion
  7.7 0.0 copy-start.1
  7.7 1.5 %fusion.29 = (bf16[16,8,8,128]{3,1,2,0:T(8,128)(2,1)S(1)}, bf16[16,8,8,128]{3,1,2,0:T(8,128)(2,1)S(1)}) fusion(f32[16,8,8,128]{3,1,0,2:T(8,128)} %get-tuple-element.15, f32[16,8,8,128]{3,1,0,2:T(8,128)S(1)} %get-tuple-element.12, f32[8,128]{1,0:T(8,128)S(1)} %broadcast_multiply_fusion, f32[16,8,8,128]{3,1,0,2:T(8,128)} %get-tuple-element.13, ...), kind=kLoop, calls=%fused_computation.47 | loop fusion | flops 786432 | bytes 2625536 | tf_op jit(solution)/shard_map/convert_element_type | solution.py:38
  9.2 17.1 %all_to_all.48 = bf16[16,8,8,128]{3,1,2,0:T(8,128)(2,1)S(1)} all-to-all(bf16[16,8,8,128]{3,1,2,0:T(8,128)(2,1)S(1)} %get-tuple-element.17), channel_id=1, replica_groups=mesh['ga'=2,'row'=8,'col'=2] {'row','col'}, dimensions={0} | all-to-all | bytes 524288 | tf_op jit(solution)/shard_map/all_to_all | solution.py:44
  26.3 12.7 %all_to_all.49 = bf16[16,8,8,128]{3,1,2,0:T(8,128)(2,1)S(1)} all-to-all(bf16[16,8,8,128]{3,1,2,0:T(8,128)(2,1)S(1)} %get-tuple-element.16), channel_id=1, replica_groups=mesh['ga'=2,'row'=8,'col'=2] {'row','col'}, dimensions={0} | all-to-all | bytes 524288 | tf_op jit(solution)/shard_map/all_to_all | solution.py:43
  39.0 0.0 copy-start.5
  39.0 0.3 fusion.3
  39.3 0.9 %copy.59 = bf16[1,8,128,128]{3,1,0,2:T(8,128)(2,1)} copy(bf16[1,8,128,128]{3,2,1,0:T(8,128)(2,1)S(1)} %fusion.3) | data formatting | bytes 524288 | tf_op jit(solution)/shard_map/convert_element_type | solution.py:51
  40.2 3.5 %all-to-all-start.2 = ((bf16[1,8,128,128]{3,1,0,2:T(8,128)(2,1)}), bf16[1,8,128,128]{3,1,0,2:T(8,128)(2,1)S(1)}, u32[]{:S(2)}, u32[]{:S(2)}) async-start(bf16[1,8,128,128]{3,1,0,2:T(8,128)(2,1)} %copy.59), calls=%async_computation.2 | async-start | bytes 524288 | tf_op jit(solution)/shard_map/all_to_all | solution.py:50
  43.7 0.0 copy-done.1
  43.8 1.8 %all_gather.7 = bf16[128,128]{1,0:T(8,128)(2,1)S(1)} all-gather(bf16[64,128]{1,0:T(8,128)(2,1)S(1)} %copy-done.1), channel_id=1, replica_groups=mesh['ga'=2,'row'=8,'col'=2] {'col'}, dimensions={0}, use_global_device_ids=true | all-gather | bytes 49152 | tf_op jit(solution)/shard_map/all_gather | solution.py:64
  45.6 8.1 %all-to-all-done.2 = bf16[1,8,128,128]{3,1,0,2:T(8,128)(2,1)S(1)} async-done(((bf16[1,8,128,128]{3,1,0,2:T(8,128)(2,1)}), bf16[1,8,128,128]{3,1,0,2:T(8,128)(2,1)S(1)}, u32[]{:S(2)}, u32[]{:S(2)}) %all-to-all-start.2) | async-done | bytes 262176 | tf_op jit(solution)/shard_map/all_to_all | solution.py:50
  53.7 0.1 fusion.30
  53.9 0.1 multiply_reduce_fusion
  54.0 0.0 copy-start.3
  54.1 0.3 fusion.27
  54.5 0.0 copy-done.5
  54.5 0.3 fusion.4
  54.8 0.0 copy-done
  54.8 0.0 copy-done.3
  54.8 0.2 fusion.47
  55.0 0.0 copy-start.2
  55.0 0.2 copy.65
  55.2 0.9 %reshape.121 = bf16[16,2,2048]{2,1,0:T(2,128)(2,1)} reshape(bf16[128,8,64]{2,1,0:T(8,128)(2,1)S(1)} %bitcast.103) | data formatting | bytes 262144
  56.1 3.5 %all-to-all-start.3 = ((bf16[16,2,2048]{2,1,0:T(2,128)(2,1)}), bf16[16,2,2048]{2,1,0:T(2,128)(2,1)S(1)}, u32[]{:S(2)}, u32[]{:S(2)}) async-start(bf16[16,2,2048]{2,1,0:T(2,128)(2,1)} %reshape.121), calls=%async_computation.3 | async-start | bytes 262144 | tf_op jit(solution)/shard_map/all_to_all | solution.py:74
  59.6 0.9 %copy.69 = bf16[8,128,128]{2,1,0:T(8,128)(2,1)} copy(bf16[8,128,128]{1,2,0:T(8,128)(2,1)S(1)} %fusion.4) | data formatting | bytes 524288
  60.5 7.0 %all-to-all-done.3 = bf16[16,2,2048]{2,1,0:T(2,128)(2,1)S(1)} async-done(((bf16[16,2,2048]{2,1,0:T(2,128)(2,1)}), bf16[16,2,2048]{2,1,0:T(2,128)(2,1)S(1)}, u32[]{:S(2)}, u32[]{:S(2)}) %all-to-all-start.3) | async-done | bytes 131104 | tf_op jit(solution)/shard_map/all_to_all | solution.py:74
  67.5 0.2 reshape.122
  67.8 0.2 copy.68
  68.1 0.0 copy-done.2
  68.1 0.1 exponential_reduce_fusion
  68.2 0.7 subtract_multiply_fusion
  (11 shorter events, 0.3 us)
Async XLA Ops:
  0.6 54.2 %copy-start = (bf16[128,64]{0,1:T(8,128)(2,1)S(1)}, bf16[128,64]{0,1:T(8,128)(2,1)}, u32[]{:S(2)}) copy-start(bf16[128,64]{0,1:T(8,128)(2,1)} %param.20) | copy-start | bytes 49156
  6.2 1.3 %copy-start.4 = (s32[128]{0:T(128)S(1)}, s32[128]{0:T(128)}, u32[]{:S(2)}) copy-start(s32[128]{0:T(128)} %param.12) | copy-start | bytes 1540
  7.7 36.0 %copy-start.1 = (bf16[64,128]{1,0:T(8,128)(2,1)S(1)}, bf16[64,128]{1,0:T(8,128)(2,1)}, u32[]{:S(2)}) copy-start(bf16[64,128]{1,0:T(8,128)(2,1)} %param.18) | copy-start | bytes 49156
  39.0 15.4 %copy-start.5 = (f32[128]{0:T(128)S(1)}, f32[128]{0:T(128)}, u32[]{:S(2)}) copy-start(f32[128]{0:T(128)} %param.19) | copy-start | bytes 1540
  40.2 13.5 %all-to-all-start.2 = ((bf16[1,8,128,128]{3,1,0,2:T(8,128)(2,1)}), bf16[1,8,128,128]{3,1,0,2:T(8,128)(2,1)S(1)}, u32[]{:S(2)}, u32[]{:S(2)}) async-start(bf16[1,8,128,128]{3,1,0,2:T(8,128)(2,1)} %copy.59), calls=%async_computation.2 | async-start | bytes 524288 | tf_op jit(solution)/shard_map/all_to_all | solution.py:50
  54.0 0.8 %copy-start.3 = (f32[64]{0:T(128)S(1)}, f32[64]{0:T(128)}, u32[]{:S(2)}) copy-start(f32[64]{0:T(128)} %param.21) | copy-start | bytes 772
  55.0 13.1 %copy-start.2 = (s32[8,128]{1,0:T(8,128)S(1)}, s32[8,128]{1,0:T(8,128)}, u32[]{:S(2)}) copy-start(s32[8,128]{1,0:T(8,128)} %param.13) | copy-start | bytes 12292
  56.1 11.4 %all-to-all-start.3 = ((bf16[16,2,2048]{2,1,0:T(2,128)(2,1)}), bf16[16,2,2048]{2,1,0:T(2,128)(2,1)S(1)}, u32[]{:S(2)}, u32[]{:S(2)}) async-start(bf16[16,2,2048]{2,1,0:T(2,128)(2,1)} %reshape.121), calls=%async_computation.3 | async-start | bytes 262144 | tf_op jit(solution)/shard_map/all_to_all | solution.py:74
where the time goes:
time: 69.3 us; the launch traced here: 68.8 us
  blocking collectives  33.9 us (49%)
  waiting for transfers between devices  15.2 us (22%)
  starting transfers between devices  7.04 us (10%)
  local copies, waits for them, and re-layouts  5.29 us (8%)
  other arithmetic  4.54 us (7%)
  matrix products  2.07 us (3%)
  between operations  0.87 us (1%)
    all_to_all x1, blocking collectives, local(): lax.all_to_all(right_blocks, ('row', 'col'), split_axis=0, concat_axis=2,...  17.1 us
    all_to_all x1, blocking collectives, local(): lax.all_to_all(left_blocks, ('row', 'col'), split_axis=0, concat_axis=2,...  12.7 us
    all_to_all x1, waiting for transfers between devices, local(): lax.all_to_all(product.astype(jnp.bfloat16), ('row', 'col'), split_axis=2...  8.14 us
    all_to_all x1, waiting for transfers between devices, local(): lax.all_to_all(logits.astype(jnp.bfloat16), ('row', 'col'), split_axis=1,...  7.02 us
    all_to_all x1, starting transfers between devices, local(): lax.all_to_all(product.astype(jnp.bfloat16), ('row', 'col'), split_axis=2...  3.53 us
    all_to_all x1, starting transfers between devices, local(): lax.all_to_all(logits.astype(jnp.bfloat16), ('row', 'col'), split_axis=1,...  3.51 us
    unnamed x16, local copies, waits for them, and re-layouts  3.09 us
    all_gather x1, blocking collectives, local(): lax.all_gather(w_in, 'col', axis=2, tiled=True)  2.27 us
  transfers between devices with their start and end apart: 2, of which 2 were waited for; matrix products, arithmetic and copies ran while one was open for 1% of the time, Pallas kernels for 0%

commit v1 on v0

v1 whole, which is shorter than its diff:
```python
import functools

import jax
import jax.numpy as jnp
from jax import lax
from jax.experimental import pallas as pl
from jax.experimental.pallas import tpu as pltpu
from jax.sharding import PartitionSpec as P

SUPER = 2
CHUNKS = 2
F32, BF16 = jnp.float32, jnp.bfloat16
NT = (((1,), (1,)), ((), ()))
TN = (((0,), (0,)), ((), ()))


def dot(lhs, rhs, dims=(((1,), (0,)), ((), ()))):
    return lax.dot_general(lhs, rhs, dims, preferred_element_type=F32)


def kernel(
    rows_n, cols_n, sup, chunks,
    pair, mask, targets, ln_gain, ln_shift, w_in, b_in, w_out, b_out, head_w, head_b,
    update, loss,
    wt, wo, normed, side_f, right_b, left_b, left_in, right_in, prod, outer, outer_f, gate,
    new_pair, logit_b, logit_in, logit_f, own_t,
    w_send, w_recv, l_send, l_recv, r_send, r_recv, o_send, o_recv, m_send, m_recv,
):
    groups = rows_n * cols_n
    count, length, width = pair.shape
    bins = head_w.shape[0]
    per = groups // sup
    share = width // per
    part = share // chunks
    half = w_in.shape[1]
    lanes = 128
    spans = length // lanes
    packed = 128 // bins
    quads = count // packed
    col = lax.axis_index("col")
    me = lax.axis_index("row") * cols_n + col
    block, slot = me // per, me % per

    def where(peer):
        return {"row": peer // cols_n, "col": peer % cols_n}

    def remote(src, dst, send, recv, peer):
        return pltpu.make_async_remote_copy(
            src_ref=src, dst_ref=dst, send_sem=send, recv_sem=recv,
            device_id=where(peer), device_id_type=pl.DeviceIdType.MESH,
        )

    def each(n, body):
        lax.fori_loop(0, n, lambda i, c: (body(i), c)[1], 0)

    barrier = pltpu.get_barrier_semaphore()

    def greet(d):
        pl.semaphore_signal(
            barrier, inc=1, device_id=where((me + 1 + d) % groups),
            device_id_type=pl.DeviceIdType.MESH,
        )

    each(groups - 1, greet)

    mine = pl.ds(pl.multiple_of(col * half, half), half)
    wt[:, mine, :] = w_in[...]
    wo[mine, :] = w_out[...]

    def norm_rows(i):
        values = pair[i].astype(F32)
        centred = values - jnp.mean(values, axis=-1, keepdims=True)
        spread = jnp.mean(centred * centred, axis=-1, keepdims=True)
        scaled = centred * lax.rsqrt(spread + 0.1) * ln_gain[0:1, :] + ln_shift[0:1, :]
        normed[i] = scaled.astype(BF16)

    each(count, norm_rows)

    row_mask = mask[...].astype(F32)
    lane = lax.broadcasted_iota(jnp.int32, (count, length), 1)
    sub = lax.broadcasted_iota(jnp.int32, (count, length), 0)
    own_mask = jnp.sum(jnp.where(lane == me * count + sub, row_mask, 0.0), axis=1, keepdims=True)
    pair_mask = own_mask * row_mask

    small = jnp.concatenate(
        [b_in[...], ln_gain[1:2, :], ln_shift[1:2, :], jnp.zeros((1, width), F32)], axis=0
    ).T

    pl.semaphore_wait(barrier, groups - 1)

    def weight_copies(peer_col):
        peer = me - col + peer_col
        return (
            remote(wt.at[:, mine, :], wt.at[:, mine, :], w_send.at[0, peer_col], w_recv.at[0, col], peer),
            remote(wo.at[mine, :], wo.at[mine, :], w_send.at[1, peer_col], w_recv.at[1, col], peer),
        )

    for d in range(1, cols_n):
        for copy in weight_copies((col + d) % cols_n):
            copy.start()

    def wait_weights(which):
        for d in range(1, cols_n):
            peer_col = (col + d) % cols_n
            theirs = pl.ds(pl.multiple_of(peer_col * half, half), half)
            ref = (wt.at[:, theirs, :], wo.at[theirs, :])[which]
            mine_ref = (wt.at[:, mine, :], wo.at[mine, :])[which]
            peer = me - col + peer_col
            remote(ref, ref, w_send.at[which, peer_col], w_recv.at[which, peer_col], peer).wait_recv()
            remote(mine_ref, mine_ref, w_send.at[which, peer_col], w_recv.at[which, peer_col], peer).wait_send()

    wait_weights(0)

    def make_side(first, out):
        weights = wt[first:first + 2].reshape(2 * width, width)
        value_b, gate_b = small[:, first:first + 1], small[:, first + 1:first + 2]

        for i in range(count):
            both = dot(weights, normed[i], NT)
            value = jax.nn.sigmoid(both[width:] + gate_b) * (both[:width] + value_b)
            for b in range(spans):
                side_f[b, pl.ds(i, width, stride=count), :] = value[:, b * lanes:(b + 1) * lanes]
        for b in range(spans):
            span = slice(b * lanes, (b + 1) * lanes)
            masked = side_f[b].reshape(width, count, lanes) * pair_mask[:, span][None]
            out[:, :, span] = masked.astype(BF16)

    def channels(owner, ch):
        return pl.ds(owner * share + ch * part, part)

    def left_copy(dest, ch):
        return remote(
            left_b.at[channels(dest, ch)],
            left_in.at[pl.ds(ch * part, part), pl.ds(slot * count, count), :],
            l_send.at[ch, dest], l_recv.at[ch, slot], block * per + dest,
        )

    def right_copy(dest, ch):
        return remote(
            right_b.at[channels(dest % per, ch)],
            right_in.at[pl.ds(ch * part, part), pl.ds(me * count, count), :],
            r_send.at[ch, dest], r_recv.at[ch, me], dest,
        )

    def right_local(ch):
        return pltpu.make_async_copy(
            right_b.at[channels(slot, ch)],
            right_in.at[pl.ds(ch * part, part), pl.ds(me * count, count), :],
            r_recv.at[ch, me],
        )

    def left_local(ch):
        return pltpu.make_async_copy(
            left_b.at[channels(slot, ch)],
            left_in.at[pl.ds(ch * part, part), pl.ds(slot * count, count), :],
            l_recv.at[ch, slot],
        )

    def send_right(ch):
        each(groups - 1, lambda d: right_copy((me + 1 + d) % groups, ch).start())
        right_local(ch).start()

    def send_left(ch):
        each(per - 1, lambda d: left_copy((slot + 1 + d) % per, ch).start())
        left_local(ch).start()

    make_side(2, right_b)
    send_right(0)
    make_side(0, left_b)
    send_left(0)
    for ch in range(1, chunks):
        send_right(ch)
        send_left(ch)

    def make_gate(i):
        gate[i] = jax.nn.sigmoid(dot(normed[i], wt[4], NT) + b_in[4:5, :])

    each(count, make_gate)
    wait_weights(1)

    def outer_copy(dest, ch):
        return remote(
            prod.at[pl.ds(ch * part, part), pl.ds(dest * count, count), :],
            outer.at[channels(slot, ch)],
            o_send.at[ch, dest], o_recv.at[ch, slot], block * per + dest,
        )

    def outer_local(ch):
        return pltpu.make_async_copy(
            prod.at[pl.ds(ch * part, part), pl.ds(slot * count, count), :],
            outer.at[channels(slot, ch)],
            o_recv.at[ch, slot],
        )

    for ch in range(chunks):
        def got_left(d):
            source = (slot + 1 + d) % per
            ref = left_in.at[pl.ds(ch * part, part), pl.ds(source * count, count), :]
            remote(ref, ref, l_send.at[ch, source], l_recv.at[ch, source], block * per + source).wait_recv()

        def got_right(d):
            source = (me + 1 + d) % groups
            ref = right_in.at[pl.ds(ch * part, part), pl.ds(source * count, count), :]
            remote(ref, ref, r_send.at[ch, source], r_recv.at[ch, source], source).wait_recv()

        each(per - 1, got_left)
        each(groups - 1, got_right)
        left_local(ch).wait()
        right_local(ch).wait()
        for c in range(ch * part, (ch + 1) * part):
            prod[c] = dot(left_in[c], right_in[c], NT).astype(BF16)
        each(per - 1, lambda d: outer_copy((slot + 1 + d) % per, ch).start())
        outer_local(ch).start()

    for ch in range(chunks):
        def got_outer(d):
            source = (slot + 1 + d) % per
            ref = outer.at[channels(source, ch)]
            remote(ref, ref, o_send.at[ch, source], o_recv.at[ch, source], block * per + source).wait_recv()

        each(per - 1, got_outer)
        outer_local(ch).wait()

    head_t = head_w[...]
    blank = jnp.zeros((bins, width), BF16)
    spread_w = [
        jnp.concatenate([head_t if h == p else blank for h in range(packed)], axis=0)
        for p in range(packed)
    ]
    bias_row = jnp.concatenate([head_b[...]] * packed, axis=1)

    gain_col, shift_col = small[:, 5:6], small[:, 6:7]
    for b in range(spans):
        span = slice(b * lanes, (b + 1) * lanes)
        values = outer[:, :, span].astype(F32)
        average = jnp.sum(values, axis=0) * (1.0 / width)
        outer_f[b] = values.reshape(width * count, lanes)
        centred = values - average[None]
        inverse = lax.rsqrt(jnp.sum(centred * centred, axis=0) * (1.0 / width) + 1.0)
        for i in range(count):
            part_i = outer_f[b, pl.ds(i, width, stride=count), :]
            part_i = (part_i - average[i:i + 1, :]) * inverse[i:i + 1, :] * gain_col + shift_col
            mixed = dot(part_i.astype(BF16), wo[...], TN) + b_out[...]
            rounded = (gate[i, span, :] * mixed).astype(BF16)
            update[i, span, :] = rounded
            new_pair[i, span, :] = (pair[i, span, :].astype(F32) + rounded.astype(F32)).astype(BF16)
    for i in range(quads):
        total = bias_row
        for p in range(packed):
            total = total + dot(new_pair[p * quads + i], spread_w[p], NT)
        logit_b[i] = total.astype(BF16)

    def logit_copy(dest):
        return remote(
            logit_b.at[:, pl.ds(dest * count, count), :], logit_in.at[me],
            m_send.at[dest], m_recv.at[me], dest,
        )

    logit_local = pltpu.make_async_copy(
        logit_b.at[:, pl.ds(me * count, count), :], logit_in.at[me], m_recv.at[me]
    )
    each(groups - 1, lambda d: logit_copy((me + 1 + d) % groups).start())
    logit_local.start()

    bias_col = jnp.concatenate([head_b[...], jnp.zeros((7, bins), F32)], axis=0).T[:, 0:1]
    for i in range(count):
        own_t[i] = dot(head_t, new_pair[i], NT) + bias_col
    at = lax.broadcasted_iota(jnp.int32, (length, length), 0)
    to = lax.broadcasted_iota(jnp.int32, (length, length), 1)
    fold = length // packed
    order = ((at % fold) // quads) * count + (at // fold) * quads + at % quads
    shuffle = jnp.where(order == to, 1.0, 0.0).astype(BF16)

    def got_logit(d):
        source = (me + 1 + d) % groups
        remote(logit_in.at[source], logit_in.at[source], m_send.at[source], m_recv.at[source], source).wait_recv()

    each(groups - 1, got_logit)
    logit_local.wait()
    logit_f[...] = logit_in[...].astype(F32).reshape(logit_f.shape)
    bin_id = lax.broadcasted_iota(jnp.int32, (bins, length), 0)
    for i in range(count):
        flipped = logit_f[pl.ds(i, groups * quads, stride=count), :].T
        flipped = jnp.concatenate([flipped[p * bins:(p + 1) * bins] for p in range(packed)], axis=1)
        symmetric = own_t[i] + dot(flipped.astype(BF16), shuffle)
        top = jnp.max(symmetric, axis=0, keepdims=True)
        total = top + jnp.log(jnp.sum(jnp.exp(symmetric - top), axis=0, keepdims=True))
        chosen = jnp.sum(jnp.where(bin_id == targets[i:i + 1, :], symmetric, 0.0), axis=0, keepdims=True)
        loss[i:i + 1, :] = pair_mask[i:i + 1, :] * (total - chosen)

    for ch in range(chunks):
        each(per - 1, lambda d: left_copy((slot + 1 + d) % per, ch).wait_send())
        each(groups - 1, lambda d: right_copy((me + 1 + d) % groups, ch).wait_send())
        each(per - 1, lambda d: outer_copy((slot + 1 + d) % per, ch).wait_send())
    each(groups - 1, lambda d: logit_copy((me + 1 + d) % groups).wait_send())


def local(rows_n, cols_n, *args):
    pair, residue_mask, targets, ln_gain, ln_shift, w_in, b_in, w_out, b_out, head_w, head_b = args
    count, length, width = pair.shape
    bins = head_w.shape[1]
    groups = rows_n * cols_n
    sup = SUPER
    per = groups // sup
    share = width // per
    chunks = CHUNKS
    packed = 128 // bins
    quads = count // packed
    dma = pltpu.SemaphoreType.DMA
    vmem = pl.BlockSpec(memory_space=pltpu.VMEM)
    return pl.pallas_call(
        functools.partial(kernel, rows_n, cols_n, sup, chunks),
        out_shape=(
            jax.ShapeDtypeStruct(pair.shape, BF16),
            jax.ShapeDtypeStruct((count, length), F32),
        ),
        in_specs=[vmem] * 11,
        out_specs=(vmem, vmem),
        scratch_shapes=[
            pltpu.VMEM((5, width, width), BF16),
            pltpu.VMEM((width, width), BF16),
            pltpu.VMEM((count, length, width), BF16),
            pltpu.VMEM((length // 128, width * count, 128), F32),
            pltpu.VMEM((width, count, length), BF16),
            pltpu.VMEM((width, count, length), BF16),
            pltpu.VMEM((share, per * count, length), BF16),
            pltpu.VMEM((share, length, length), BF16),
            pltpu.VMEM((share, per * count, length), BF16),
            pltpu.VMEM((width, count, length), BF16),
            pltpu.VMEM((length // 128, width * count, 128), F32),
            pltpu.VMEM((count, length, width), F32),
            pltpu.VMEM((count, length, width), BF16),
            pltpu.VMEM((quads, length, 128), BF16),
            pltpu.VMEM((groups, quads, count, 128), BF16),
            pltpu.VMEM((groups * quads * count, 128), F32),
            pltpu.VMEM((count, bins, length), F32),
            dma((2, cols_n)), dma((2, cols_n)),
            dma((chunks, per)), dma((chunks, per)),
            dma((chunks, groups)), dma((chunks, groups)),
            dma((chunks, per)), dma((chunks, per)),
            dma((groups,)), dma((groups,)),
        ],
        compiler_params=pltpu.CompilerParams(
            collective_id=0, has_side_effects=True, vmem_limit_bytes=60 * 1024 * 1024
        ),
    )(
        pair, residue_mask.reshape(1, length), targets, ln_gain, ln_shift,
        jnp.swapaxes(w_in, 1, 2), b_in, w_out, b_out.reshape(1, width), head_w.T, head_b.reshape(1, bins),
    )


def solution(mesh):
    placed = (
        P(("ga", "row", "col"), None, None),
        P("ga"),
        P(("ga", "row", "col"), None),
        P(),
        P(),
        P(None, None, "col"),
        P(),
        P("col", None),
        P(),
        P(),
        P(),
    )
    return jax.shard_map(
        functools.partial(local, mesh.shape["row"], mesh.shape["col"]),
        mesh=mesh,
        in_specs=placed,
        out_specs=(P(("ga", "row", "col"), None, None), P(("ga", "row", "col"), None)),
        check_vma=False,
    )
```

time: 69.3 us -> 37.9 us (0.55)
  Pallas kernels: 0 us -> 34.9 us
  blocking collectives: 33.9 us -> 0 us
  waiting for transfers between devices: 15.2 us -> 0 us
  starting transfers between devices: 7.04 us -> 0 us
  other arithmetic: 4.54 us -> 0 us
  local copies, waits for them, and re-layouts: 5.29 us -> 2.27 us
  matrix products: 2.07 us -> 0 us
    pallas_call x0 -> x1, Pallas kernels: none -> 34.9 us  [local(): pl.pallas_call(functools.partial(kernel, rows_n, cols_n, sup, chunks), ou...]
    all_to_all x2 -> x0, blocking collectives: 29.8 us -> none  [the longest x1 17.1 us: local(): lax.all_to_all(right_blocks, ('row', 'col'), split_axis=0, concat_axis=2,...]
    all_to_all x2 -> x0, waiting for transfers between devices: 15.2 us -> none  [the longest x1 8.14 us: local(): lax.all_to_all(product.astype(jnp.bfloat16), ('row', 'col'), split_axis=2...]
    all_to_all x2 -> x0, starting transfers between devices: 7.04 us -> none  [the longest x1 3.53 us: local(): lax.all_to_all(product.astype(jnp.bfloat16), ('row', 'col'), split_axis=2...]
    all_gather x2 -> x0, blocking collectives: 4.1 us -> none  [the longest x1 2.27 us: local(): lax.all_gather(w_in, 'col', axis=2, tiled=True)]
    dot_general x4 -> x0, matrix products: 2.07 us -> none  [the longest x1 1.27 us: local(): jnp.einsum('ikc,ncd->ndik', normed, lax.all_gather(w_in, 'col', axis=2, t...]
    convert_element_type x4 -> x0, other arithmetic: 1.89 us -> none  [the longest x1 1.52 us: local(): left_side = stacked[0].astype(jnp.bfloat16)]
    div x3 -> x0, other arithmetic: 1.31 us -> none  [the longest x1 1.3 us: local(): left_side = pair_mask * jax.nn.sigmoid(projected[1]) * projected[0]]
  transfers between devices with their start and end apart: 2 -> 0, of which waited for: 2 -> 0; matrix products, arithmetic and copies ran while one was open for 1% -> 0% of each run, Pallas kernels for 0% -> 0%
where the time goes in v1:
time: 37.9 us; the launch traced here: 37.8 us
  Pallas kernels  34.9 us (92%)
  local copies, waits for them, and re-layouts  2.27 us (6%)
  between operations  0.65 us (2%)
    pallas_call x1, Pallas kernels, local(): pl.pallas_call(functools.partial(kernel, rows_n, cols_n, sup, chunks), ou...  34.9 us
    unnamed x4, local copies, waits for them, and re-layouts  2.27 us

profile of v1, /device:TPU:0, one launch (start us, length us, event | category | flops | bytes accessed | tf_op | source)
XLA Modules:
  0.0 37.8 jit_solution(3036982261653250908)
XLA Ops:
  0.6 34.9 %shard_map.122 = (bf16[8,128,128]{2,1,0:T(8,128)(2,1)}, f32[8,128]{1,0:T(8,128)}) custom-call(bf16[8,128,128]{2,1,0:T(8,128)(2,1)} %pair.1, s32[1,128]{1,0:T(1,128)} %bitcast.7, s32[8,128]{1,0:T(8,128)} %targets.1, f32[2,128]{1,0:T(2,128)} %ln_gain.1, f32[2,128]{1,0:T(2,128)} %ln_shift.1, bf16[5,64,128]{2,1,0:T(8,128)(2,1)} %bitcast.5, f32[5,128]{1,0:T(8,128)} %b_in.1, ...), custom_call_target="tpu_custom_call" | custom-call | tf_op jit(solution)/shard_map/pallas_call | solution.py:311
  35.5 0.0 copy-start
  35.5 1.7 %copy.15 = bf16[8,128,128]{2,1,0:T(8,128)(2,1)} copy(bf16[8,128,128]{2,1,0:T(8,128)(2,1)} %get-tuple-element.4) | data formatting | bytes 524288
  37.2 0.0 copy-done
  37.2 0.6 %copy.16 = f32[8,128]{1,0:T(8,128)} copy(f32[8,128]{1,0:T(8,128)S(1)} %copy-done) | data formatting | bytes 8192
Async XLA Ops:
  35.5 1.7 %copy-start = (f32[8,128]{1,0:T(8,128)S(1)}, f32[8,128]{1,0:T(8,128)}, u32[]{:S(2)}) copy-start(f32[8,128]{1,0:T(8,128)} %get-tuple-element.5) | copy-start | bytes 12292

commit v2 on v1

--- a/solution.py
+++ b/solution.py
@@ -22,7 +22,7 @@
     rows_n, cols_n, sup, chunks,
     pair, mask, targets, ln_gain, ln_shift, w_in, b_in, w_out, b_out, head_w, head_b,
     update, loss,
-    wt, wo, normed, side_f, right_b, left_b, left_in, right_in, prod, outer, outer_f, gate,
+    wt, wo, small, normed, side_f, right_b, left_b, left_in, right_in, prod, outer, outer_f, gate,
     new_pair, logit_b, logit_in, logit_f, own_t,
     w_send, w_recv, l_send, l_recv, r_send, r_recv, o_send, o_recv, m_send, m_recv,
 ):
@@ -51,7 +51,7 @@
         )
 
     def each(n, body):
-        lax.fori_loop(0, n, lambda i, c: (body(i), c)[1], 0)
+        lax.fori_loop(0, n, lambda i, c: (body(i), c)[1], 0, unroll=True)
 
     barrier = pltpu.get_barrier_semaphore()
 
@@ -82,7 +82,7 @@
     own_mask = jnp.sum(jnp.where(lane == me * count + sub, row_mask, 0.0), axis=1, keepdims=True)
     pair_mask = own_mask * row_mask
 
-    small = jnp.concatenate(
+    small[...] = jnp.concatenate(
         [b_in[...], ln_gain[1:2, :], ln_shift[1:2, :], jnp.zeros((1, width), F32)], axis=0
     ).T
 
@@ -109,21 +109,21 @@
             remote(ref, ref, w_send.at[which, peer_col], w_recv.at[which, peer_col], peer).wait_recv()
             remote(mine_ref, mine_ref, w_send.at[which, peer_col], w_recv.at[which, peer_col], peer).wait_send()
 
-    wait_weights(0)
-
-    def make_side(first, out):
-        weights = wt[first:first + 2].reshape(2 * width, width)
-        value_b, gate_b = small[:, first:first + 1], small[:, first + 1:first + 2]
+    def make_side(first, out, span_w):
+        start = pl.multiple_of(span_w * half, half)
+        rows = pl.ds(start, half)
+        weights = wt[first:first + 2, rows, :].reshape(2 * half, width)
+        value_b, gate_b = small[rows, first:first + 1], small[rows, first + 1:first + 2]
 
         for i in range(count):
             both = dot(weights, normed[i], NT)
-            value = jax.nn.sigmoid(both[width:] + gate_b) * (both[:width] + value_b)
+            value = jax.nn.sigmoid(both[half:] + gate_b) * (both[:half] + value_b)
             for b in range(spans):
-                side_f[b, pl.ds(i, width, stride=count), :] = value[:, b * lanes:(b + 1) * lanes]
+                side_f[b, pl.ds(i, half, stride=count), :] = value[:, b * lanes:(b + 1) * lanes]
         for b in range(spans):
             span = slice(b * lanes, (b + 1) * lanes)
-            masked = side_f[b].reshape(width, count, lanes) * pair_mask[:, span][None]
-            out[:, :, span] = masked.astype(BF16)
+            masked = side_f[b].reshape(half, count, lanes) * pair_mask[:, span][None]
+            out[rows, :, span] = masked.astype(BF16)
 
     def channels(owner, ch):
         return pl.ds(owner * share + ch * part, part)
@@ -131,46 +131,73 @@
     def left_copy(dest, ch):
         return remote(
             left_b.at[channels(dest, ch)],
-            left_in.at[pl.ds(ch * part, part), pl.ds(slot * count, count), :],
+            left_in.at[slot, pl.ds(ch * part, part)],
             l_send.at[ch, dest], l_recv.at[ch, slot], block * per + dest,
         )
 
     def right_copy(dest, ch):
         return remote(
             right_b.at[channels(dest % per, ch)],
-            right_in.at[pl.ds(ch * part, part), pl.ds(me * count, count), :],
+            right_in.at[me, pl.ds(ch * part, part)],
             r_send.at[ch, dest], r_recv.at[ch, me], dest,
         )
 
     def right_local(ch):
         return pltpu.make_async_copy(
             right_b.at[channels(slot, ch)],
-            right_in.at[pl.ds(ch * part, part), pl.ds(me * count, count), :],
+            right_in.at[me, pl.ds(ch * part, part)],
             r_recv.at[ch, me],
         )
 
     def left_local(ch):
         return pltpu.make_async_copy(
             left_b.at[channels(slot, ch)],
-            left_in.at[pl.ds(ch * part, part), pl.ds(slot * count, count), :],
+            left_in.at[slot, pl.ds(ch * part, part)],
             l_recv.at[ch, slot],
         )
 
-    def send_right(ch):
-        each(groups - 1, lambda d: right_copy((me + 1 + d) % groups, ch).start())
+    quota = per // cols_n
+
+    def send_right(ch, span_w):
+        def one(d):
+            owner = span_w * quota + (slot + d) % quota
+            dest = (block * per + owner + (d // quota) * per) % groups
+
+            @pl.when(dest != me)
+            def _():
+                right_copy(dest, ch).start()
+
+        each(sup * quota, one)
+
+    def send_left(ch, span_w):
+        def one(d):
+            owner = span_w * quota + (slot + d) % quota
+
+            @pl.when(owner != slot)
+            def _():
+                left_copy(owner, ch).start()
+
+        each(quota, one)
+
+    for turn in range(cols_n):
+        if turn == 1:
+            wait_weights(0)
+        span_w = (col + turn) % cols_n
+        make_side(2, right_b, span_w)
+        send_right(0, span_w)
+    right_local(0).start()
+    for turn in range(cols_n):
+        span_w = (col + turn) % cols_n
+        make_side(0, left_b, span_w)
+        send_left(0, span_w)
+    left_local(0).start()
+    for ch in range(1, chunks):
+        for turn in range(cols_n):
+            send_right(ch, (col + turn) % cols_n)
         right_local(ch).start()
-
-    def send_left(ch):
-        each(per - 1, lambda d: left_copy((slot + 1 + d) % per, ch).start())
+        for turn in range(cols_n):
+            send_left(ch, (col + turn) % cols_n)
         left_local(ch).start()
-
-    make_side(2, right_b)
-    send_right(0)
-    make_side(0, left_b)
-    send_left(0)
-    for ch in range(1, chunks):
-        send_right(ch)
-        send_left(ch)
 
     def make_gate(i):
         gate[i] = jax.nn.sigmoid(dot(normed[i], wt[4], NT) + b_in[4:5, :])
@@ -180,14 +207,14 @@
 
     def outer_copy(dest, ch):
         return remote(
-            prod.at[pl.ds(ch * part, part), pl.ds(dest * count, count), :],
+            prod.at[dest, pl.ds(ch * part, part)],
             outer.at[channels(slot, ch)],
             o_send.at[ch, dest], o_recv.at[ch, slot], block * per + dest,
         )
 
     def outer_local(ch):
         return pltpu.make_async_copy(
-            prod.at[pl.ds(ch * part, part), pl.ds(slot * count, count), :],
+            prod.at[slot, pl.ds(ch * part, part)],
             outer.at[channels(slot, ch)],
             o_recv.at[ch, slot],
         )
@@ -195,12 +222,12 @@
     for ch in range(chunks):
         def got_left(d):
             source = (slot + 1 + d) % per
-            ref = left_in.at[pl.ds(ch * part, part), pl.ds(source * count, count), :]
+            ref = left_in.at[source, pl.ds(ch * part, part)]
             remote(ref, ref, l_send.at[ch, source], l_recv.at[ch, source], block * per + source).wait_recv()
 
         def got_right(d):
             source = (me + 1 + d) % groups
-            ref = right_in.at[pl.ds(ch * part, part), pl.ds(source * count, count), :]
+            ref = right_in.at[source, pl.ds(ch * part, part)]
             remote(ref, ref, r_send.at[ch, source], r_recv.at[ch, source], source).wait_recv()
 
         each(per - 1, got_left)
@@ -208,7 +235,9 @@
         left_local(ch).wait()
         right_local(ch).wait()
         for c in range(ch * part, (ch + 1) * part):
-            prod[c] = dot(left_in[c], right_in[c], NT).astype(BF16)
+            lhs = left_in[:, c].reshape(per * count, length)
+            rhs = right_in[:, c].reshape(length, length)
+            prod[:, c] = dot(lhs, rhs, NT).astype(BF16).reshape(per, count, length)
         each(per - 1, lambda d: outer_copy((slot + 1 + d) % per, ch).start())
         outer_local(ch).start()
 
@@ -248,16 +277,16 @@
         total = bias_row
         for p in range(packed):
             total = total + dot(new_pair[p * quads + i], spread_w[p], NT)
-        logit_b[i] = total.astype(BF16)
+        logit_b[:, i] = total.astype(BF16).reshape(groups, count, 128)
 
     def logit_copy(dest):
         return remote(
-            logit_b.at[:, pl.ds(dest * count, count), :], logit_in.at[me],
+            logit_b.at[dest], logit_in.at[me],
             m_send.at[dest], m_recv.at[me], dest,
         )
 
     logit_local = pltpu.make_async_copy(
-        logit_b.at[:, pl.ds(me * count, count), :], logit_in.at[me], m_recv.at[me]
+        logit_b.at[me], logit_in.at[me], m_recv.at[me]
     )
     each(groups - 1, lambda d: logit_copy((me + 1 + d) % groups).start())
     logit_local.start()
@@ -319,18 +348,19 @@
         scratch_shapes=[
             pltpu.VMEM((5, width, width), BF16),
             pltpu.VMEM((width, width), BF16),
+            pltpu.VMEM((width, 8), F32),
             pltpu.VMEM((count, length, width), BF16),
-            pltpu.VMEM((length // 128, width * count, 128), F32),
+            pltpu.VMEM((length // 128, width // cols_n * count, 128), F32),
             pltpu.VMEM((width, count, length), BF16),
             pltpu.VMEM((width, count, length), BF16),
-            pltpu.VMEM((share, per * count, length), BF16),
-            pltpu.VMEM((share, length, length), BF16),
-            pltpu.VMEM((share, per * count, length), BF16),
+            pltpu.VMEM((per, share, count, length), BF16),
+            pltpu.VMEM((groups, share, count, length), BF16),
+            pltpu.VMEM((per, share, count, length), BF16),
             pltpu.VMEM((width, count, length), BF16),
             pltpu.VMEM((length // 128, width * count, 128), F32),
             pltpu.VMEM((count, length, width), F32),
             pltpu.VMEM((count, length, width), BF16),
-            pltpu.VMEM((quads, length, 128), BF16),
+            pltpu.VMEM((groups, quads, count, 128), BF16),
             pltpu.VMEM((groups, quads, count, 128), BF16),
             pltpu.VMEM((groups * quads * count, 128), F32),
             pltpu.VMEM((count, bins, length), F32),

time: 37.9 us -> 35.5 us (0.937)
  Pallas kernels: 34.9 us -> 32.4 us
    pallas_call x1, Pallas kernels: 34.9 us -> 32.4 us  [local(): pl.pallas_call(functools.partial(kernel, rows_n, cols_n, sup, chunks), ou...]
where the time goes in v2:
time: 35.5 us; the launch traced here: 35.3 us
  Pallas kernels  32.4 us (91%)
  local copies, waits for them, and re-layouts  2.27 us (6%)
  between operations  0.65 us (2%)
    pallas_call x1, Pallas kernels, local(): pl.pallas_call(functools.partial(kernel, rows_n, cols_n, sup, chunks), ou...  32.4 us
    unnamed x4, local copies, waits for them, and re-layouts  2.27 us

profile of v2, /device:TPU:0, one launch (start us, length us, event | category | flops | bytes accessed | tf_op | source)
XLA Modules:
  0.0 35.3 jit_solution(10127850051928136946)
XLA Ops:
  0.6 32.4 %shard_map.122 = (bf16[8,128,128]{2,1,0:T(8,128)(2,1)}, f32[8,128]{1,0:T(8,128)}) custom-call(bf16[8,128,128]{2,1,0:T(8,128)(2,1)} %pair.1, s32[1,128]{1,0:T(1,128)} %bitcast.7, s32[8,128]{1,0:T(8,128)} %targets.1, f32[2,128]{1,0:T(2,128)} %ln_gain.1, f32[2,128]{1,0:T(2,128)} %ln_shift.1, bf16[5,64,128]{2,1,0:T(8,128)(2,1)} %bitcast.5, f32[5,128]{1,0:T(8,128)} %b_in.1, ...), custom_call_target="tpu_custom_call" | custom-call | tf_op jit(solution)/shard_map/pallas_call | solution.py:340
  33.0 0.0 copy-start
  33.0 1.7 %copy.15 = bf16[8,128,128]{2,1,0:T(8,128)(2,1)} copy(bf16[8,128,128]{2,1,0:T(8,128)(2,1)} %get-tuple-element.4) | data formatting | bytes 524288
  34.7 0.0 copy-done
  34.7 0.6 %copy.16 = f32[8,128]{1,0:T(8,128)} copy(f32[8,128]{1,0:T(8,128)S(1)} %copy-done) | data formatting | bytes 8192
Async XLA Ops:
  33.0 1.7 %copy-start = (f32[8,128]{1,0:T(8,128)S(1)}, f32[8,128]{1,0:T(8,128)}, u32[]{:S(2)}) copy-start(f32[8,128]{1,0:T(8,128)} %get-tuple-element.5) | copy-start | bytes 12292

commit v3 on v2

--- a/solution.py
+++ b/solution.py
@@ -9,6 +9,7 @@
 
 SUPER = 2
 CHUNKS = 2
+EIGHTHS = 4
 F32, BF16 = jnp.float32, jnp.bfloat16
 NT = (((1,), (1,)), ((), ()))
 TN = (((0,), (0,)), ((), ()))
@@ -20,18 +21,24 @@
 
 def kernel(
     rows_n, cols_n, sup, chunks,
-    pair, mask, targets, ln_gain, ln_shift, w_in, b_in, w_out, b_out, head_w, head_b,
-    update, loss,
+    *refs,
+):
+    sources, (update_out, loss) = refs[:11], refs[11:13]
+    held, rest = refs[13:24], refs[24:]
+    (pair, mask, targets, ln_gain, ln_shift, w_in, b_in, w_out, b_out, head_w, head_b) = held
+    (
     wt, wo, small, normed, side_f, right_b, left_b, left_in, right_in, prod, outer, outer_f, gate,
-    new_pair, logit_b, logit_in, logit_f, own_t,
-    w_send, w_recv, l_send, l_recv, r_send, r_recv, o_send, o_recv, m_send, m_recv,
-):
+        new_pair, logit_b, logit_in, logit_f, own_t,
+        w_send, w_recv, l_send, l_recv, r_send, r_recv, o_send, o_recv, m_send, m_recv,
+        in_sem, out_sem, update,
+    ) = rest
     groups = rows_n * cols_n
     count, length, width = pair.shape
     bins = head_w.shape[0]
     per = groups // sup
     share = width // per
-    part = share // chunks
+    first = max(share * EIGHTHS // 8, 1)
+    edges = [0, first, share] if chunks > 1 else [0, share]
     half = w_in.shape[1]
     lanes = 128
     spans = length // lanes
@@ -39,10 +46,10 @@
     quads = count // packed
     col = lax.axis_index("col")
     me = lax.axis_index("row") * cols_n + col
-    block, slot = me // per, me % per
+    block, slot = lax.div(me, per), lax.rem(me, per)
 
     def where(peer):
-        return {"row": peer // cols_n, "col": peer % cols_n}
+        return {"row": lax.div(peer, cols_n), "col": lax.rem(peer, cols_n)}
 
     def remote(src, dst, send, recv, peer):
         return pltpu.make_async_remote_copy(
@@ -53,16 +60,25 @@
     def each(n, body):
         lax.fori_loop(0, n, lambda i, c: (body(i), c)[1], 0, unroll=True)
 
+    loads = [pltpu.make_async_copy(sources[n], held[n], in_sem.at[n]) for n in range(11)]
+    for load in loads:
+        load.start()
     barrier = pltpu.get_barrier_semaphore()
 
     def greet(d):
         pl.semaphore_signal(
-            barrier, inc=1, device_id=where((me + 1 + d) % groups),
+            barrier, inc=1, device_id=where(lax.rem(me + 1 + d, groups)),
             device_id_type=pl.DeviceIdType.MESH,
         )
 
     each(groups - 1, greet)
 
+    def drain(ref, sem):
+        pltpu.make_async_copy(ref, ref, sem).wait()
+
+
+    for load in loads:
+        load.wait()
     mine = pl.ds(pl.multiple_of(col * half, half), half)
     wt[:, mine, :] = w_in[...]
     wo[mine, :] = w_out[...]
@@ -96,12 +112,12 @@
         )
 
     for d in range(1, cols_n):
-        for copy in weight_copies((col + d) % cols_n):
+        for copy in weight_copies(lax.rem(col + d, cols_n)):
             copy.start()
 
     def wait_weights(which):
         for d in range(1, cols_n):
-            peer_col = (col + d) % cols_n
+            peer_col = lax.rem(col + d, cols_n)
             theirs = pl.ds(pl.multiple_of(peer_col * half, half), half)
             ref = (wt.at[:, theirs, :], wo.at[theirs, :])[which]
             mine_ref = (wt.at[:, mine, :], wo.at[mine, :])[which]
@@ -126,42 +142,42 @@
             out[rows, :, span] = masked.astype(BF16)
 
     def channels(owner, ch):
-        return pl.ds(owner * share + ch * part, part)
+        return pl.ds(owner * share + edges[ch], edges[ch + 1] - edges[ch])
 
     def left_copy(dest, ch):
         return remote(
             left_b.at[channels(dest, ch)],
-            left_in.at[slot, pl.ds(ch * part, part)],
-            l_send.at[ch, dest], l_recv.at[ch, slot], block * per + dest,
+            left_in.at[slot, pl.ds(edges[ch], edges[ch + 1] - edges[ch])],
+            l_send.at[ch], l_recv.at[ch], block * per + dest,
         )
 
     def right_copy(dest, ch):
         return remote(
-            right_b.at[channels(dest % per, ch)],
-            right_in.at[me, pl.ds(ch * part, part)],
-            r_send.at[ch, dest], r_recv.at[ch, me], dest,
+            right_b.at[channels(lax.rem(dest, per), ch)],
+            right_in.at[me, pl.ds(edges[ch], edges[ch + 1] - edges[ch])],
+            r_send.at[ch], r_recv.at[ch], dest,
         )
 
     def right_local(ch):
         return pltpu.make_async_copy(
             right_b.at[channels(slot, ch)],
-            right_in.at[me, pl.ds(ch * part, part)],
-            r_recv.at[ch, me],
+            right_in.at[me, pl.ds(edges[ch], edges[ch + 1] - edges[ch])],
+            r_recv.at[ch],
         )
 
     def left_local(ch):
         return pltpu.make_async_copy(
             left_b.at[channels(slot, ch)],
-            left_in.at[slot, pl.ds(ch * part, part)],
-            l_recv.at[ch, slot],
+            left_in.at[slot, pl.ds(edges[ch], edges[ch + 1] - edges[ch])],
+            l_recv.at[ch],
         )
 
     quota = per // cols_n
 
     def send_right(ch, span_w):
         def one(d):
-            owner = span_w * quota + (slot + d) % quota
-            dest = (block * per + owner + (d // quota) * per) % groups
+            owner = span_w * quota + lax.rem(slot + d, quota)
+            dest = lax.rem(block * per + owner + lax.div(d, quota) * per, groups)
 
             @pl.when(dest != me)
             def _():
@@ -171,7 +187,7 @@
 
     def send_left(ch, span_w):
         def one(d):
-            owner = span_w * quota + (slot + d) % quota
+            owner = span_w * quota + lax.rem(slot + d, quota)
 
             @pl.when(owner != slot)
             def _():
@@ -182,21 +198,21 @@
     for turn in range(cols_n):
         if turn == 1:
             wait_weights(0)
-        span_w = (col + turn) % cols_n
+        span_w = lax.rem(col + turn, cols_n)
         make_side(2, right_b, span_w)
         send_right(0, span_w)
     right_local(0).start()
     for turn in range(cols_n):
-        span_w = (col + turn) % cols_n
+        span_w = lax.rem(col + turn, cols_n)
         make_side(0, left_b, span_w)
         send_left(0, span_w)
     left_local(0).start()
     for ch in range(1, chunks):
         for turn in range(cols_n):
-            send_right(ch, (col + turn) % cols_n)
+            send_right(ch, lax.rem(col + turn, cols_n))
         right_local(ch).start()
         for turn in range(cols_n):
-            send_left(ch, (col + turn) % cols_n)
+            send_left(ch, lax.rem(col + turn, cols_n))
         left_local(ch).start()
 
     def make_gate(i):
@@ -207,48 +223,31 @@
 
     def outer_copy(dest, ch):
         return remote(
-            prod.at[dest, pl.ds(ch * part, part)],
+            prod.at[dest, pl.ds(edges[ch], edges[ch + 1] - edges[ch])],
             outer.at[channels(slot, ch)],
-            o_send.at[ch, dest], o_recv.at[ch, slot], block * per + dest,
+            o_send.at[ch], o_recv.at[ch], block * per + dest,
         )
 
     def outer_local(ch):
         return pltpu.make_async_copy(
-            prod.at[slot, pl.ds(ch * part, part)],
+            prod.at[slot, pl.ds(edges[ch], edges[ch + 1] - edges[ch])],
             outer.at[channels(slot, ch)],
-            o_recv.at[ch, slot],
+            o_recv.at[ch],
         )
 
     for ch in range(chunks):
-        def got_left(d):
-            source = (slot + 1 + d) % per
-            ref = left_in.at[source, pl.ds(ch * part, part)]
-            remote(ref, ref, l_send.at[ch, source], l_recv.at[ch, source], block * per + source).wait_recv()
-
-        def got_right(d):
-            source = (me + 1 + d) % groups
-            ref = right_in.at[source, pl.ds(ch * part, part)]
-            remote(ref, ref, r_send.at[ch, source], r_recv.at[ch, source], source).wait_recv()
-
-        each(per - 1, got_left)
-        each(groups - 1, got_right)
-        left_local(ch).wait()
-        right_local(ch).wait()
-        for c in range(ch * part, (ch + 1) * part):
+        now = pl.ds(edges[ch], edges[ch + 1] - edges[ch])
+        drain(left_in.at[:, now], l_recv.at[ch])
+        drain(right_in.at[:, now], r_recv.at[ch])
+        for c in range(edges[ch], edges[ch + 1]):
             lhs = left_in[:, c].reshape(per * count, length)
             rhs = right_in[:, c].reshape(length, length)
             prod[:, c] = dot(lhs, rhs, NT).astype(BF16).reshape(per, count, length)
-        each(per - 1, lambda d: outer_copy((slot + 1 + d) % per, ch).start())
+        each(per - 1, lambda d: outer_copy(lax.rem(slot + 1 + d, per), ch).start())
         outer_local(ch).start()
 
     for ch in range(chunks):
-        def got_outer(d):
-            source = (slot + 1 + d) % per
-            ref = outer.at[channels(source, ch)]
-            remote(ref, ref, o_send.at[ch, source], o_recv.at[ch, source], block * per + source).wait_recv()
-
-        each(per - 1, got_outer)
-        outer_local(ch).wait()
+        drain(prod.at[:, pl.ds(edges[ch], edges[ch + 1] - edges[ch])], o_recv.at[ch])
 
     head_t = head_w[...]
     blank = jnp.zeros((bins, width), BF16)
@@ -273,6 +272,8 @@
             rounded = (gate[i, span, :] * mixed).astype(BF16)
             update[i, span, :] = rounded
             new_pair[i, span, :] = (pair[i, span, :].astype(F32) + rounded.astype(F32)).astype(BF16)
+    store = pltpu.make_async_copy(update, update_out, out_sem)
+    store.start()
     for i in range(quads):
         total = bias_row
         for p in range(packed):
@@ -282,13 +283,13 @@
     def logit_copy(dest):
         return remote(
             logit_b.at[dest], logit_in.at[me],
-            m_send.at[dest], m_recv.at[me], dest,
+            m_send.at[0], m_recv.at[0], dest,
         )
 
     logit_local = pltpu.make_async_copy(
-        logit_b.at[me], logit_in.at[me], m_recv.at[me]
+        logit_b.at[me], logit_in.at[me], m_recv.at[0]
     )
-    each(groups - 1, lambda d: logit_copy((me + 1 + d) % groups).start())
+    each(groups - 1, lambda d: logit_copy(lax.rem(me + 1 + d, groups)).start())
     logit_local.start()
 
     bias_col = jnp.concatenate([head_b[...], jnp.zeros((7, bins), F32)], axis=0).T[:, 0:1]
@@ -300,12 +301,7 @@
     order = ((at % fold) // quads) * count + (at // fold) * quads + at % quads
     shuffle = jnp.where(order == to, 1.0, 0.0).astype(BF16)
 
-    def got_logit(d):
-        source = (me + 1 + d) % groups
-        remote(logit_in.at[source], logit_in.at[source], m_send.at[source], m_recv.at[source], source).wait_recv()
-
-    each(groups - 1, got_logit)
-    logit_local.wait()
+    drain(logit_in, m_recv.at[0])
     logit_f[...] = logit_in[...].astype(F32).reshape(logit_f.shape)
     bin_id = lax.broadcasted_iota(jnp.int32, (bins, length), 0)
     for i in range(count):
@@ -318,10 +314,12 @@
         loss[i:i + 1, :] = pair_mask[i:i + 1, :] * (total - chosen)
 
     for ch in range(chunks):
-        each(per - 1, lambda d: left_copy((slot + 1 + d) % per, ch).wait_send())
-        each(groups - 1, lambda d: right_copy((me + 1 + d) % groups, ch).wait_send())
-        each(per - 1, lambda d: outer_copy((slot + 1 + d) % per, ch).wait_send())
-    each(groups - 1, lambda d: logit_copy((me + 1 + d) % groups).wait_send())
+        now = pl.ds(edges[ch], edges[ch + 1] - edges[ch])
+        drain(left_in.at[pl.ds(0, per - 1), now], l_send.at[ch])
+        drain(right_in.at[pl.ds(0, groups - 1), now], r_send.at[ch])
+        drain(prod.at[pl.ds(0, per - 1), now], o_send.at[ch])
+    drain(logit_in.at[pl.ds(0, groups - 1)], m_send.at[0])
+    store.wait()
 
 
 def local(rows_n, cols_n, *args):
@@ -337,15 +335,20 @@
     quads = count // packed
     dma = pltpu.SemaphoreType.DMA
     vmem = pl.BlockSpec(memory_space=pltpu.VMEM)
+    inputs = (
+        pair, residue_mask.reshape(1, length), targets, ln_gain, ln_shift,
+        jnp.swapaxes(w_in, 1, 2), b_in, w_out, b_out.reshape(1, width), head_w.T,
+        head_b.reshape(1, bins),
+    )
     return pl.pallas_call(
         functools.partial(kernel, rows_n, cols_n, sup, chunks),
         out_shape=(
             jax.ShapeDtypeStruct(pair.shape, BF16),
             jax.ShapeDtypeStruct((count, length), F32),
         ),
-        in_specs=[vmem] * 11,
-        out_specs=(vmem, vmem),
-        scratch_shapes=[
+        in_specs=[pl.BlockSpec(memory_space=pl.ANY)] * 11,
+        out_specs=(pl.BlockSpec(memory_space=pl.ANY), vmem),
+        scratch_shapes=[pltpu.VMEM(x.shape, x.dtype) for x in inputs] + [
             pltpu.VMEM((5, width, width), BF16),
             pltpu.VMEM((width, width), BF16),
             pltpu.VMEM((width, 8), F32),
@@ -365,18 +368,14 @@
             pltpu.VMEM((groups * quads * count, 128), F32),
             pltpu.VMEM((count, bins, length), F32),
             dma((2, cols_n)), dma((2, cols_n)),
-            dma((chunks, per)), dma((chunks, per)),
-            dma((chunks, groups)), dma((chunks, groups)),
-            dma((chunks, per)), dma((chunks, per)),
-            dma((groups,)), dma((groups,)),
+            dma((chunks,)), dma((chunks,)), dma((chunks,)), dma((chunks,)), dma((chunks,)), dma((chunks,)),
+            dma((1,)), dma((1,)),
+            dma((11,)), dma, pltpu.VMEM(pair.shape, BF16),
         ],
         compiler_params=pltpu.CompilerParams(
             collective_id=0, has_side_effects=True, vmem_limit_bytes=60 * 1024 * 1024
         ),
-    )(
-        pair, residue_mask.reshape(1, length), targets, ln_gain, ln_shift,
-        jnp.swapaxes(w_in, 1, 2), b_in, w_out, b_out.reshape(1, width), head_w.T, head_b.reshape(1, bins),
-    )
+    )(*inputs)
 
 
 def solution(mesh):

time: 35.5 us -> 33.3 us (0.938)
  Pallas kernels: 32.4 us -> 30.2 us
    pallas_call x1, Pallas kernels: 32.4 us -> 30.2 us  [local(): pl.pallas_call(functools.partial(kernel, rows_n, cols_n, sup, chunks), ou...]
where the time goes in v3:
time: 33.3 us; the launch traced here: 33.1 us
  Pallas kernels  30.2 us (91%)
  local copies, waits for them, and re-layouts  2.27 us (7%)
  between operations  0.65 us (2%)
    pallas_call x1, Pallas kernels, local(): pl.pallas_call(functools.partial(kernel, rows_n, cols_n, sup, chunks), ou...  30.2 us
    unnamed x4, local copies, waits for them, and re-layouts  2.27 us

profile of v3, /device:TPU:0, one launch (start us, length us, event | category | flops | bytes accessed | tf_op | source)
XLA Modules:
  0.0 33.1 jit_solution(9056582669135820472)
XLA Ops:
  0.6 30.2 %shard_map.122 = (bf16[8,128,128]{2,1,0:T(8,128)(2,1)}, f32[8,128]{1,0:T(8,128)}) custom-call(bf16[8,128,128]{2,1,0:T(8,128)(2,1)} %refs_0_.1, s32[1,128]{1,0:T(1,128)} %bitcast.7, s32[8,128]{1,0:T(8,128)} %refs_2_.1, f32[2,128]{1,0:T(2,128)} %refs_3_.1, f32[2,128]{1,0:T(2,128)} %refs_4_.1, bf16[5,64,128]{2,1,0:T(8,128)(2,1)} %bitcast.5, f32[5,128]{1,0:T(8,128)} %refs_6_.1, ...), custom_call_target="tpu_custom_call" | custom-call | tf_op jit(solution)/shard_map/pallas_call | solution.py:343
  30.9 0.0 copy-start
  30.9 1.7 %copy.15 = bf16[8,128,128]{2,1,0:T(8,128)(2,1)} copy(bf16[8,128,128]{2,1,0:T(8,128)(2,1)} %get-tuple-element.4) | data formatting | bytes 524288
  32.5 0.0 copy-done
  32.5 0.6 %copy.16 = f32[8,128]{1,0:T(8,128)} copy(f32[8,128]{1,0:T(8,128)S(1)} %copy-done) | data formatting | bytes 8192
Async XLA Ops:
  30.9 1.7 %copy-start = (f32[8,128]{1,0:T(8,128)S(1)}, f32[8,128]{1,0:T(8,128)}, u32[]{:S(2)}) copy-start(f32[8,128]{1,0:T(8,128)} %get-tuple-element.5) | copy-start | bytes 12292

commit v4 on v3

--- a/solution.py
+++ b/solution.py
@@ -23,14 +23,14 @@
     rows_n, cols_n, sup, chunks,
     *refs,
 ):
-    sources, (update_out, loss) = refs[:11], refs[11:13]
+    sources, (update, loss) = refs[:11], refs[11:13]
     held, rest = refs[13:24], refs[24:]
     (pair, mask, targets, ln_gain, ln_shift, w_in, b_in, w_out, b_out, head_w, head_b) = held
     (
     wt, wo, small, normed, side_f, right_b, left_b, left_in, right_in, prod, outer, outer_f, gate,
         new_pair, logit_b, logit_in, logit_f, own_t,
         w_send, w_recv, l_send, l_recv, r_send, r_recv, o_send, o_recv, m_send, m_recv,
-        in_sem, out_sem, update,
+        in_sem,
     ) = rest
     groups = rows_n * cols_n
     count, length, width = pair.shape
@@ -272,8 +272,6 @@
             rounded = (gate[i, span, :] * mixed).astype(BF16)
             update[i, span, :] = rounded
             new_pair[i, span, :] = (pair[i, span, :].astype(F32) + rounded.astype(F32)).astype(BF16)
-    store = pltpu.make_async_copy(update, update_out, out_sem)
-    store.start()
     for i in range(quads):
         total = bias_row
         for p in range(packed):
@@ -319,7 +317,6 @@
         drain(right_in.at[pl.ds(0, groups - 1), now], r_send.at[ch])
         drain(prod.at[pl.ds(0, per - 1), now], o_send.at[ch])
     drain(logit_in.at[pl.ds(0, groups - 1)], m_send.at[0])
-    store.wait()
 
 
 def local(rows_n, cols_n, *args):
@@ -343,11 +340,11 @@
     return pl.pallas_call(
         functools.partial(kernel, rows_n, cols_n, sup, chunks),
         out_shape=(
-            jax.ShapeDtypeStruct(pair.shape, BF16),
-            jax.ShapeDtypeStruct((count, length), F32),
+            pltpu.VMEM(pair.shape, BF16),
+            pltpu.VMEM((count, length), F32),
         ),
         in_specs=[pl.BlockSpec(memory_space=pl.ANY)] * 11,
-        out_specs=(pl.BlockSpec(memory_space=pl.ANY), vmem),
+        out_specs=(vmem, vmem),
         scratch_shapes=[pltpu.VMEM(x.shape, x.dtype) for x in inputs] + [
             pltpu.VMEM((5, width, width), BF16),
             pltpu.VMEM((width, width), BF16),
@@ -370,7 +367,7 @@
             dma((2, cols_n)), dma((2, cols_n)),
             dma((chunks,)), dma((chunks,)), dma((chunks,)), dma((chunks,)), dma((chunks,)), dma((chunks,)),
             dma((1,)), dma((1,)),
-            dma((11,)), dma, pltpu.VMEM(pair.shape, BF16),
+            dma((11,)),
         ],
         compiler_params=pltpu.CompilerParams(
             collective_id=0, has_side_effects=True, vmem_limit_bytes=60 * 1024 * 1024

time: 33.3 us -> 31.7 us (0.952)
  local copies, waits for them, and re-layouts: 2.27 us -> 1.3 us
  Pallas kernels: 30.2 us -> 29.6 us
    unnamed x4 -> x2, local copies, waits for them, and re-layouts: 2.27 us -> 1.3 us
    pallas_call x1, Pallas kernels: 30.2 us -> 29.6 us  [local(): pl.pallas_call(functools.partial(kernel, rows_n, cols_n, sup, chunks), ou...]
where the time goes in v4:
time: 31.7 us; the launch traced here: 31.6 us
  Pallas kernels  29.6 us (93%)
  local copies, waits for them, and re-layouts  1.3 us (4%)
  between operations  0.64 us (2%)
    pallas_call x1, Pallas kernels, local(): pl.pallas_call(functools.partial(kernel, rows_n, cols_n, sup, chunks), ou...  29.6 us
    unnamed x2, local copies, waits for them, and re-layouts  1.3 us

profile of v4, /device:TPU:0, one launch (start us, length us, event | category | flops | bytes accessed | tf_op | source)
XLA Modules:
  0.0 31.6 jit_solution(582090295916394782)
XLA Ops:
  0.6 29.6 %shard_map.122 = (bf16[8,128,128]{2,1,0:T(8,128)(2,1)S(1)}, f32[8,128]{1,0:T(8,128)S(1)}) custom-call(bf16[8,128,128]{2,1,0:T(8,128)(2,1)} %refs_0_.1, s32[1,128]{1,0:T(1,128)} %bitcast.7, s32[8,128]{1,0:T(8,128)} %refs_2_.1, f32[2,128]{1,0:T(2,128)} %refs_3_.1, f32[2,128]{1,0:T(2,128)} %refs_4_.1, bf16[5,64,128]{2,1,0:T(8,128)(2,1)} %bitcast.5, ...), custom_call_target="tpu_custom_call" | custom-call | tf_op jit(solution)/shard_map/pallas_call | solution.py:340
  30.3 0.7 %copy.15 = bf16[8,128,128]{2,1,0:T(8,128)(2,1)} copy(bf16[8,128,128]{2,1,0:T(8,128)(2,1)S(1)} %get-tuple-element.2) | data formatting | bytes 524288
  31.0 0.6 %copy.16 = f32[8,128]{1,0:T(8,128)} copy(f32[8,128]{1,0:T(8,128)S(1)} %get-tuple-element.3) | data formatting | bytes 8192
